TPU v7x, 128 devices: a whole 4x4x4 slice. The times are simulated.
128 devices in a mesh: dp: 2 (over core), ep: 64 (over x, y, z).
Axes of the slice: x: 4, y: 4, z: 4, core: 2. Of those that a mesh axis runs over, the one named last changes fastest.
Arguments:
- x: bfloat16 [2, 64, 256, 1792], P('dp', 'ep'), parts along dimension 0
- expert: int32 [2, 64, 256, 8], P('dp', 'ep'), parts along dimension 0
- slot: int32 [2, 64, 256, 8], P('dp', 'ep'), parts along dimension 0
- gate: float32 [2, 64, 256, 8], P('dp', 'ep'), parts along dimension 0
- w_gate: bfloat16 [64, 1792, 2560], P('ep')
- w_up: bfloat16 [64, 1792, 2560], P('ep')
- w_down: bfloat16 [64, 2560, 1792], P('ep')
- s_gate: bfloat16 [1792, 20480], replicated
- s_up: bfloat16 [1792, 20480], replicated
- s_down: bfloat16 [20480, 1792], replicated
Outputs:
- y: bfloat16 [2, 64, 256, 1792], P('dp', 'ep'), parts along dimension 0
There are 2 independent parts. A program takes and returns all parts, laid end to end along the dimension named above; an argument that names none is the same for every part.
All inputs are finite; a program needn't handle non-finite values.
Results may differ from a plain program's by a relative error of at most 0.009.
Values are sent between devices in bfloat16 or wider.
A program may use at most 1.5 GiB of HBM per device.

v0:
```python
import jax
import jax.numpy as jnp
from jax import lax
from jax.sharding import NamedSharding, PartitionSpec as P


def einsum(form, a, b):
    return jnp.einsum(form, a.astype(jnp.float32), b.astype(jnp.float32))


def for_all(x, s_gate, s_up, s_down):
    h = jax.nn.silu(einsum("...d,df->...f", x, s_gate)) * einsum("...d,df->...f", x, s_up)
    return einsum("...f,fd->...d", h.astype(jnp.bfloat16), s_down)


def solution(mesh):
    def placed(v, *spec):
        return lax.with_sharding_constraint(v, NamedSharding(mesh, P(*spec)))

    def step(x, expert, slot, gate, w_gate, w_up, w_down, s_gate, s_up, s_down):
        experts, (tokens, top) = w_gate.shape[0], expert.shape[2:]
        slots = 5 * tokens * top // (4 * experts)
        to_expert = jax.nn.one_hot(expert, experts, dtype=jnp.bfloat16)
        to_slot = jax.nn.one_hot(slot, slots, dtype=jnp.bfloat16)
        weighted = to_expert * gate[..., None].astype(jnp.bfloat16)
        dispatch = einsum("abtke,abtkc->abtec", to_expert, to_slot).astype(jnp.bfloat16)
        combine = einsum("abtke,abtkc->abtec", weighted, to_slot).astype(jnp.bfloat16)
        z = einsum("abtec,abtd->aebcd", dispatch, x).astype(jnp.bfloat16)
        z = placed(z, "dp", None, "ep", None, None)
        z = placed(z, "dp", "ep", None, None, None)
        h = jax.nn.silu(einsum("aebcd,edf->aebcf", z, w_gate))
        h = (h * einsum("aebcd,edf->aebcf", z, w_up)).astype(jnp.bfloat16)
        out = einsum("aebcf,efd->aebcd", h, w_down).astype(jnp.bfloat16)
        out = placed(out, "dp", "ep", None, None, None)
        out = placed(out, "dp", None, "ep", None, None)
        y = einsum("abtec,aebcd->abtd", combine, out)
        return (y + for_all(x, s_gate, s_up, s_down)).astype(jnp.bfloat16)

    return step
```

profile of v0, /device:TPU:39, one launch (start us, length us, event | category | flops | bytes accessed | tf_op | source)
XLA Modules:
  0.0 430.0 jit_solution(678763739991628438)
XLA Ops:
  0.0 0.0 copy-start
  0.0 0.9 copy.4
  0.9 0.0 copy-start.2
  0.9 0.8 copy.6
  1.8 0.0 copy-done.2
  1.8 0.0 copy-start.3
  1.8 0.6 copy-done.3
  2.4 3.6 fusion.48
  6.0 5.6 %copy.11 = bf16[256,64,40]{0,2,1:T(8,128)(2,1)S(1)} copy(bf16[256,64,40]{1,2,0:T(8,128)(2,1)} %fusion.48) | data formatting | bytes 2621440 | tf_op jit(solution)/abtke,abtkc->abtec/dot_general | solution.py:8
  11.7 0.0 copy-done
  11.7 6.0 %convert_bitcast_fusion.1 = bf16[1,64,1,1,40,1792]{5,4,3,2,0,1:T(8,128)(2,1)} fusion(bf16[256,64,40]{0,2,1:T(8,128)(2,1)S(1)} %copy.11, bf16[1,1,256,1792]{3,2,1,0:T(8,128)(2,1)S(1)} %copy-done), kind=kOutput, calls=%fused_computation.25 | convolution fusion | flops 2353397760 | bytes 11403264 | tf_op jit(solution)/abtec,abtd->aebcd/dot_general | solution.py:8
  17.7 0.0 copy-start.4
  17.7 10.9 %all-to-all-start = ((bf16[1,64,1,1,40,1792]{5,4,3,2,0,1:T(8,128)(2,1)}), bf16[1,64,1,1,40,1792]{5,4,3,2,0,1:T(8,128)(2,1)}, u32[]{:S(2)}, u32[]{:S(2)}) async-start(bf16[1,64,1,1,40,1792]{5,4,3,2,0,1:T(8,128)(2,1)} %convert_bitcast_fusion.1), calls=%async_computation | async-start | bytes 18350080 | tf_op jit(solution)/sharding_constraint;jit(solution)/sharding_constraint | solution.py:18
  28.7 0.0 copy-done.4
  28.7 0.7 copy.5
  29.4 4.3 %fusion.52 = bf16[256,64,40]{1,2,0:T(8,128)(2,1)S(1)} fusion(s32[256,8]{1,0:T(8,128)} %copy-done.3, s32[256,8]{1,0:T(8,128)} %copy-done.2, bf16[256,8]{1,0:T(8,128)(2,1)} %copy.5), kind=kOutput, calls=%fused_computation.39 | convolution fusion | flops 10829824 | bytes 1331200 | tf_op jit(solution)/abtke,abtkc->abtec/dot_general | solution.py:8
  33.8 3.5 copy.10
  37.3 38.2 %convolution_bitcast_fusion.1 = f32[1,1,256,20480]{3,2,1,0:T(8,128)} fusion(bf16[1792,20480]{1,0:T(8,128)(2,1)} %param.7, bf16[1,1,256,1792]{3,2,1,0:T(8,128)(2,1)S(1)} %copy-done), kind=kOutput, calls=%fused_computation.1 | convolution fusion | flops 18790481920 | bytes 95289344 | tf_op jit(solution)/...d,df->...f/dot_general | solution.py:8
  75.4 96.2 %all-to-all-done = bf16[1,64,1,1,40,1792]{5,4,3,2,0,1:T(8,128)(2,1)} async-done(((bf16[1,64,1,1,40,1792]{5,4,3,2,0,1:T(8,128)(2,1)}), bf16[1,64,1,1,40,1792]{5,4,3,2,0,1:T(8,128)(2,1)}, u32[]{:S(2)}, u32[]{:S(2)}) %all-to-all-start) | async-done | bytes 9175072 | tf_op jit(solution)/sharding_constraint;jit(solution)/sharding_constraint | solution.py:18
  171.6 31.5 %fusion.17 = f32[64,40,2560]{2,1,0:T(8,128)} fusion(bf16[1,1792,2560]{2,1,0:T(8,128)(2,1)} %param.4, bf16[1,64,1,1,40,1792]{5,4,3,2,0,1:T(8,128)(2,1)} %all-to-all-done), kind=kOutput, calls=%fused_computation.19 | convolution fusion | flops 23488102400 | bytes 44564480 | tf_op jit(solution)/aebcd,edf->aebcf/dot_general | solution.py:8
  203.2 0.0 copy-start.5
  203.2 33.5 %fusion.88 = bf16[64,40,2560]{2,1,0:T(8,128)(2,1)} fusion(f32[64,40,2560]{2,1,0:T(8,128)} %fusion.17, bf16[1,1792,2560]{2,1,0:T(8,128)(2,1)} %param.5, bf16[1,64,1,1,40,1792]{5,4,3,2,0,1:T(8,128)(2,1)} %all-to-all-done), kind=kOutput, calls=%fused_computation.13.clone.clone.clone.1 | convolution fusion | flops 23527424000 | bytes 57671680 | tf_op jit(solution)/aebcd,edf->aebcf/dot_general | solution.py:8
  236.6 0.0 copy-done.5
  236.6 27.5 %convert_bitcast_fusion = bf16[1,1,64,1,40,1792]{5,4,3,1,0,2:T(8,128)(2,1)} fusion(bf16[1,2560,1792]{2,1,0:T(8,128)(2,1)S(1)} %copy-done.5, bf16[64,40,2560]{2,1,0:T(8,128)(2,1)} %fusion.88), kind=kOutput, calls=%fused_computation.24 | convolution fusion | flops 23492689920 | bytes 31457280 | tf_op jit(solution)/aebcf,efd->aebcd/dot_general | solution.py:8
  264.2 7.9 %all-to-all-start.1 = ((bf16[1,1,64,1,40,1792]{5,4,3,1,0,2:T(8,128)(2,1)}), bf16[1,1,64,1,40,1792]{5,4,3,1,0,2:T(8,128)(2,1)}, u32[]{:S(2)}, u32[]{:S(2)}) async-start(bf16[1,1,64,1,40,1792]{5,4,3,1,0,2:T(8,128)(2,1)} %convert_bitcast_fusion), calls=%async_computation.1 | async-start | bytes 18350080 | tf_op jit(solution)/sharding_constraint;jit(solution)/sharding_constraint | solution.py:18
  272.1 37.0 %fusion.6.clone.4 = bf16[256,20480]{1,0:T(8,128)(2,1)} fusion(bf16[1792,20480]{1,0:T(8,128)(2,1)} %param.8, f32[1,1,256,20480]{3,2,1,0:T(8,128)} %convolution_bitcast_fusion.1, bf16[1,1,256,1792]{3,2,1,0:T(8,128)(2,1)S(1)} %copy-done), kind=kOutput, calls=%fused_computation.11.clone.clone.clone.1 | convolution fusion | flops 18821939200 | bytes 105775104 | tf_op jit(solution)/...d,df->...f/dot_general | solution.py:8
  309.2 0.0 copy-start.1
  309.2 31.4 %fusion.31 = f32[256,1792]{1,0:T(8,128)} fusion(bf16[20480,1792]{1,0:T(8,128)(2,1)} %param.9, bf16[256,20480]{1,0:T(8,128)(2,1)} %fusion.6.clone.4), kind=kOutput, calls=%fused_computation.26 | convolution fusion | flops 18790481920 | bytes 85721088 | tf_op jit(solution)/...f,fd->...d/dot_general | solution.py:8
  340.6 81.8 %all-to-all-done.1 = bf16[1,1,64,1,40,1792]{5,4,3,1,0,2:T(8,128)(2,1)} async-done(((bf16[1,1,64,1,40,1792]{5,4,3,1,0,2:T(8,128)(2,1)}), bf16[1,1,64,1,40,1792]{5,4,3,1,0,2:T(8,128)(2,1)}, u32[]{:S(2)}, u32[]{:S(2)}) %all-to-all-start.1) | async-done | bytes 9175072 | tf_op jit(solution)/sharding_constraint;jit(solution)/sharding_constraint | solution.py:18
  422.4 0.0 copy-done.1
  422.4 7.6 %fusion.41 = bf16[1,1,256,1792]{3,2,1,0:T(8,128)(2,1)} fusion(f32[256,1792]{1,0:T(8,128)} %fusion.31, bf16[1,1,64,1,40,1792]{5,4,3,1,0,2:T(8,128)(2,1)} %all-to-all-done.1, bf16[256,64,40]{0,1,2:T(8,128)(2,1)S(1)} %copy-done.1), kind=kOutput, calls=%fused_computation.30 | convolution fusion | flops 2349727744 | bytes 13238272 | tf_op jit(solution)/abtec,aebcd->abtd/dot_general | solution.py:8
  (1 shorter events, 0.0 us)
Async XLA Ops:
  0.0 11.7 %copy-start = (bf16[1,1,256,1792]{3,2,1,0:T(8,128)(2,1)S(1)}, bf16[1,1,256,1792]{3,2,1,0:T(8,128)(2,1)}, u32[]{:S(2)}) copy-start(bf16[1,1,256,1792]{3,2,1,0:T(8,128)(2,1)} %param.3) | copy-start | bytes 2752516
  0.9 0.9 copy-start.2
  1.8 0.7 copy-start.3
  17.7 11.0 %copy-start.4 = (f32[1,1,256,8]{2,3,1,0:T(8,128)S(1)}, f32[1,1,256,8]{2,3,1,0:T(8,128)}, u32[]{:S(2)}) copy-start(f32[1,1,256,8]{2,3,1,0:T(8,128)} %param.1) | copy-start | bytes 24580
  17.7 153.9 %all-to-all-start = ((bf16[1,64,1,1,40,1792]{5,4,3,2,0,1:T(8,128)(2,1)}), bf16[1,64,1,1,40,1792]{5,4,3,2,0,1:T(8,128)(2,1)}, u32[]{:S(2)}, u32[]{:S(2)}) async-start(bf16[1,64,1,1,40,1792]{5,4,3,2,0,1:T(8,128)(2,1)} %convert_bitcast_fusion.1), calls=%async_computation | async-start | bytes 18350080 | tf_op jit(solution)/sharding_constraint;jit(solution)/sharding_constraint | solution.py:18
  203.2 33.5 %copy-start.5 = (bf16[1,2560,1792]{2,1,0:T(8,128)(2,1)S(1)}, bf16[1,2560,1792]{2,1,0:T(8,128)(2,1)}, u32[]{:S(2)}) copy-start(bf16[1,2560,1792]{2,1,0:T(8,128)(2,1)} %param.6) | copy-start | bytes 27525124
  264.2 158.2 %all-to-all-start.1 = ((bf16[1,1,64,1,40,1792]{5,4,3,1,0,2:T(8,128)(2,1)}), bf16[1,1,64,1,40,1792]{5,4,3,1,0,2:T(8,128)(2,1)}, u32[]{:S(2)}, u32[]{:S(2)}) async-start(bf16[1,1,64,1,40,1792]{5,4,3,1,0,2:T(8,128)(2,1)} %convert_bitcast_fusion), calls=%async_computation.1 | async-start | bytes 18350080 | tf_op jit(solution)/sharding_constraint;jit(solution)/sharding_constraint | solution.py:18
  309.2 113.2 %copy-start.1 = (bf16[256,64,40]{0,1,2:T(8,128)(2,1)S(1)}, bf16[256,64,40]{0,1,2:T(8,128)(2,1)}, u32[]{:S(2)}) copy-start(bf16[256,64,40]{0,1,2:T(8,128)(2,1)} %copy.10) | copy-start | bytes 3932164
where the time goes:
time: 431 us; the launch traced here: 430 us
  matrix products  221 us (51%)
  waiting for transfers between devices  178 us (41%)
  starting transfers between devices  18.9 us (4%)
  local copies, waits for them, and re-layouts  12.3 us (3%)
    dot_general x10, matrix products, einsum(): return jnp.einsum(form, a.astype(jnp.float32), b.astype(jnp.float32))  221 us
    another operation x2, waiting for transfers between devices, placed(): return lax.with_sharding_constraint(v, NamedSharding(mesh, P(*spec)))  178 us
    another operation x2, starting transfers between devices, placed(): return lax.with_sharding_constraint(v, NamedSharding(mesh, P(*spec)))  18.9 us
    dot_general x2, local copies, waits for them, and re-layouts, einsum(): return jnp.einsum(form, a.astype(jnp.float32), b.astype(jnp.float32))  9.12 us
  transfers between devices with their start and end apart: 2, of which 2 were waited for; matrix products, arithmetic and copies ran while one was open for 27% of the time, Pallas kernels for 0%

commit v1 on v0

v1 whole, which is shorter than its diff:
```python
import functools

import jax
import jax.numpy as jnp
from jax import lax
from jax.experimental import pallas as pl
from jax.experimental.pallas import tpu as pltpu
from jax.sharding import PartitionSpec as P

MESH = pl.DeviceIdType.MESH
N = 4
STRIDE = (16, 4, 1)
TURNS = ((0, 1, 2), (1, 2, 0), (2, 0, 1))
SUB = 8
F32, BF16 = jnp.float32, jnp.bfloat16


def dot(a, b):
    return jnp.dot(a, b, preferred_element_type=F32)


def kernel(cfg, *refs):
    tokens, chunks, cols, ff, f_tile, d_tile, units, u_tile, top, slots = (
        cfg["tokens"], cfg["chunks"], cfg["cols"], cfg["ff"], cfg["f_tile"], cfg["d_tile"],
        cfg["units"], cfg["u_tile"], cfg["top"], cfg["slots"])
    it = iter(refs)
    take = lambda n: [next(it) for _ in range(n)]
    x_hbm, meta, wg_hbm, wu_hbm, wd_hbm, sg_hbm, su_hbm, sd_hbm = take(8)
    (y_ref,) = take(1)
    made, bl, ecl, ebl = take(3), take(3), take(3), take(3)
    xv, = take(1)
    al = take(3)
    eal = take(3)
    met, stage, wg, wu, wd, z, h, acc, sg, su, sd = take(11)
    (x_sem, w_sem, s_sem, st_sem, a_send, a_recv, m_send, m_recv, b_send, b_recv, b_self, c_send, c_recv, c_self,
     ec_send, ec_recv, ec_self, eb_send, eb_recv, ld_sem, ea_send, ea_recv) = take(22)

    me = lax.axis_index("ep")
    co = (me // 16, lax.rem(me // 4, 4), lax.rem(me, 4))
    starts = [sum(cols[:r]) for r in range(3)]
    span = [pl.ds(starts[r], cols[r]) for r in range(3)]
    d = sum(cols)

    def hop(c, s):
        return lax.rem(c + s, N)

    def peer(axis, s):
        return {"ep": me + (hop(co[axis], s) - co[axis]) * STRIDE[axis]}

    def remote(src, dst, send, recv, to):
        return pltpu.make_async_remote_copy(
            src_ref=src, dst_ref=dst, send_sem=send, recv_sem=recv, device_id=to, device_id_type=MESH)

    def at_b(ref, r, k, b):
        return ref.at[k, :, b] if TURNS[r] == (2, 0, 1) else ref.at[k, :, :, b]

    def at_c(ref, r, k, c):
        axis = TURNS[r][2]
        if axis == 0:
            return ref.at[k, c, :, :, :, span[r]]
        if axis == 1:
            return ref.at[k, :, c, :, :, span[r]]
        return ref.at[k, :, :, c, :, span[r]]

    def a_copy(r, s):
        return remote(x_hbm.at[:, span[r]], al[r].at[3 - s], a_send.at[r, 3 - s], a_recv.at[r, 3 - s], peer(TURNS[r][0], s))

    def m_copy(axis, s):
        return remote(meta, met.at[axis, 3 - s], m_send.at[axis, 3 - s], m_recv.at[axis, 3 - s], peer(axis, s))

    def stage_copy(r, k):
        return pltpu.make_async_copy(stage.at[:, :, :, :, span[r]], made[r].at[k], st_sem.at[r])

    def b_own(r, k):
        b = co[TURNS[r][1]]
        return pltpu.make_async_copy(stage.at[b, :, :, :, span[r]], at_b(bl[r], r, k, b), b_self.at[r])

    def b_copy(r, k, s):
        b = co[TURNS[r][1]]
        return remote(made[r].at[k, hop(b, s)], at_b(bl[r], r, k, b), b_send.at[r, k, s - 1], b_recv.at[r, k, s - 1], peer(TURNS[r][1], s))

    def c_own(r, k):
        c = co[TURNS[r][2]]
        return pltpu.make_async_copy(bl[r].at[k, c], at_c(z, r, k, c), c_self.at[r, k])

    def c_copy(r, k, s):
        c = co[TURNS[r][2]]
        return remote(bl[r].at[k, hop(c, s)], at_c(z, r, k, c), c_send.at[r, k, s - 1], c_recv.at[r, k, s - 1], peer(TURNS[r][2], s))

    def ec_own(r, k):
        c = co[TURNS[r][2]]
        return pltpu.make_async_copy(at_c(z, r, k, c), ecl[r].at[k, c], ec_self.at[r, k])

    def ec_copy(r, k, s):
        c = co[TURNS[r][2]]
        return remote(at_c(z, r, k, hop(c, s)), ecl[r].at[k, c], ec_send.at[r, k, s - 1], ec_recv.at[r, k, s - 1], peer(TURNS[r][2], s))

    def eb_copy(r, k, s):
        b = co[TURNS[r][1]]
        return remote(at_b(ecl[r], r, k, hop(b, s)), ebl[r].at[k, b], eb_send.at[r, k, s - 1], eb_recv.at[r, k, s - 1], peer(TURNS[r][1], s))

    def ea_copy(r, s):
        return remote(al[r].at[s - 1], eal[r].at[3 - s], ea_send.at[r, 3 - s], ea_recv.at[r, 3 - s], peer(TURNS[r][0], s))

    def load(r, k, o):
        b = co[TURNS[r][1]]
        src = at_b(ecl[r], r, k, b) if o == 0 else ebl[r].at[k, hop(b, o)]
        return pltpu.make_async_copy(src, wd.at[k, hop(b, o), :, :, :, span[r]], ld_sem.at[r, k, o])

    hops = [(r, s) for r in range(3) for s in (1, 3, 2)]

    def s_copies(u):
        i = lax.rem(u, 2)
        w = pl.ds(pl.multiple_of(u * u_tile, u_tile), u_tile)
        return [pltpu.make_async_copy(sg_hbm.at[:, w], sg.at[i], s_sem.at[i, 0]),
                pltpu.make_async_copy(su_hbm.at[:, w], su.at[i], s_sem.at[i, 1]),
                pltpu.make_async_copy(sd_hbm.at[w, :], sd.at[i], s_sem.at[i, 2])]

    def shared(lo, hi):
        def unit(u, _):
            @pl.when(u + 1 < units)
            def _():
                for c in s_copies(u + 1):
                    c.start()
            for c in s_copies(u):
                c.wait()
            i = lax.rem(u, 2)
            g = dot(xv[...], sg[i])
            act = (jax.nn.silu(g) * dot(xv[...], su[i])).astype(BF16)
            acc[...] += dot(act, sd[i])
            return 0
        lax.fori_loop(lo, hi, unit, 0)

    def matches(r, o, first, count, weight):
        a_axis, b_axis, c_axis = TURNS[r]
        m = meta if o == 0 else met.at[a_axis, o - 1]
        i = lax.broadcasted_iota(jnp.int32, (count, tokens), 0)
        expert = co[a_axis] * STRIDE[a_axis] + ((i // 32) % 4) * STRIDE[b_axis] + ((i // 8) % 4) * STRIDE[c_axis]
        code = (expert * slots + (i // 128 + first) * SUB + i % 8).astype(F32)
        out = jnp.zeros((count, tokens), F32)
        for j in range(top):
            out = jnp.where(m[j : j + 1, :] == code, m[top + j : top + j + 1, :] if weight else 1.0, out)
        return out.astype(BF16)

    def gather(k):
        for r in range(3):
            for o in range(4):
                src = xv[:, span[r]] if o == 0 else al[r][o - 1]
                rows = dot(matches(r, o, k, 128, False), src).astype(BF16)
                stage[:, :, hop(co[TURNS[r][0]], o), :, span[r]] = rows.reshape(4, 4, SUB, cols[r])

    def forward_c(k):
        for r in range(3):
            for s in (1, 2, 3):
                b_copy(r, k, s).wait_recv()
        for r, s in hops:
            c_copy(r, k, s).start()
        for r in range(3):
            c_own(r, k).start()

    def forward_eb(k):
        for r in range(3):
            for s in (1, 2, 3):
                ec_copy(r, k, s).wait_recv()
            ec_own(r, k).wait()
        for r, s in hops:
            eb_copy(r, k, s).start()

    def weights():
        return [pltpu.make_async_copy(wg_hbm, wg, w_sem.at[0]), pltpu.make_async_copy(wu_hbm, wu, w_sem.at[1]),
                pltpu.make_async_copy(wd_hbm, wd, w_sem.at[2])]

    rows = N * N * N * SUB

    def expert(k):
        for r in range(3):
            for s in (1, 2, 3):
                c_copy(r, k, s).wait_recv()
            c_own(r, k).wait()

        def up(f, _):
            w = pl.ds(pl.multiple_of(f * f_tile, f_tile), f_tile)
            zk = z[k].reshape(rows, d)
            h[:, w] = (jax.nn.silu(dot(zk, wg[:, w])) * dot(zk, wu[:, w])).astype(BF16)
            return 0
        lax.fori_loop(0, ff // f_tile, up, 0)

        @pl.when(k >= 1)
        def _():
            forward_eb(k - 1)

        def down(n, _):
            w = pl.ds(pl.multiple_of(n * d_tile, d_tile), d_tile)
            out = dot(h[...], wd[:, :, :, :, :, w].reshape(ff, d_tile))
            z[k, :, :, :, :, w] = out.astype(BF16).reshape(N, N, N, SUB, d_tile)
            return 0
        lax.fori_loop(0, d // d_tile, down, 0)
        for r, s in hops:
            ec_copy(r, k, s).start()
        for r in range(3):
            ec_own(r, k).start()

    for c in s_copies(0):
        c.start()
    x_in = pltpu.make_async_copy(x_hbm, xv, x_sem)
    x_in.start()
    barrier = pltpu.get_barrier_semaphore()
    for axis in range(3):
        for s in (1, 2, 3):
            pl.semaphore_signal(barrier, inc=1, device_id=peer(axis, s), device_id_type=MESH)
    pl.semaphore_wait(barrier, 9)
    for axis in range(3):
        for s in (1, 3, 2):
            m_copy(axis, s).start()
    for r, s in hops:
        a_copy(r, s).start()
    acc[...] = jnp.zeros_like(acc)
    for c in weights():
        c.start()
    x_in.wait()
    plan = cfg["plan"]
    shared(0, plan[0])
    for axis in range(3):
        for s in (1, 2, 3):
            m_copy(axis, s).wait_recv()
    for r, s in hops:
        a_copy(r, s).wait_recv()

    def dispatch(k, _):
        gather(k)
        for r in range(3):
            stage_copy(r, k).start()
            b_own(r, k).start()
        for r in range(3):
            stage_copy(r, k).wait()
            b_own(r, k).wait()
        for r, s in hops:
            b_copy(r, k, s).start()
        return 0
    early = min(3, chunks)
    lax.fori_loop(0, early, dispatch, 0)

    def later(k, _):
        forward_c(k)
        @pl.when(k + early < chunks)
        def _():
            dispatch(k + early, 0)
        shared(plan[0] + k * plan[1], plan[0] + (k + 1) * plan[1])
        return 0
    lax.fori_loop(0, chunks, later, 0)
    for c in weights():
        c.wait()
    lax.fori_loop(0, chunks, lambda k, _: (expert(k), 0)[1], 0)
    done = plan[0] + chunks * plan[1]
    shared(done, done + plan[2])
    for k in range(chunks - 1):
        for r in range(3):
            for s in (1, 2, 3):
                eb_copy(r, k, s).wait_recv()
            for o in range(4):
                load(r, k, o).start()
    forward_eb(chunks - 1)
    shared(done + plan[2], units)
    for k in range(chunks - 1, chunks):
        for r in range(3):
            for s in (1, 2, 3):
                eb_copy(r, k, s).wait_recv()
            for o in range(4):
                load(r, k, o).start()
    for r in range(3):
        for k in range(chunks):
            for o in range(4):
                load(r, k, o).wait()
    for o in (2, 1, 3, 0):
        for r in range(3):
            src = wd[:, :, :, hop(co[TURNS[r][0]], o), :, span[r]]
            part = lax.dot_general(
                matches(r, o, 0, 128 * chunks, True), src.reshape(128 * chunks, cols[r]),
                (((0,), (0,)), ((), ())), preferred_element_type=F32)
            if o == 0:
                acc[:, span[r]] += part
            else:
                al[r][o - 1] = part.astype(BF16)
                ea_copy(r, o).start()
    for r, s in hops:
        ea_copy(r, s).wait_recv()
    for r in range(3):
        total = acc[:, span[r]]
        for o in range(3):
            total += eal[r][o].astype(F32)
        y_ref[:, span[r]] = total.astype(BF16)

    for axis in range(3):
        for s in (1, 2, 3):
            m_copy(axis, s).wait_send()
    for r, s in hops:
        a_copy(r, s).wait_send()
        ea_copy(r, s).wait_send()

    def drain(k, _):
        for r, s in hops:
            b_copy(r, k, s).wait_send()
            c_copy(r, k, s).wait_send()
            ec_copy(r, k, s).wait_send()
            eb_copy(r, k, s).wait_send()
        return 0
    lax.fori_loop(0, chunks, drain, 0)


def layer(x, meta, w_gate, w_up, w_down, s_gate, s_up, s_down, cfg):
    tokens, chunks, cols, ff, units, u_tile = (cfg[n] for n in ("tokens", "chunks", "cols", "ff", "units", "u_tile"))
    d, rows = sum(cols), N * N * N * SUB
    any_ = pl.BlockSpec(memory_space=pl.ANY)
    vm = pl.BlockSpec(memory_space=pltpu.VMEM)
    block = lambda w: jax.ShapeDtypeStruct((chunks, N, N, N, SUB, w), BF16)
    dma = pltpu.SemaphoreType.DMA
    phase = [dma((3, chunks, 3)), dma((3, chunks, 3))]
    outs = pl.pallas_call(
        functools.partial(kernel, cfg),
        out_shape=[jax.ShapeDtypeStruct((tokens, d), BF16)] + [block(w) for _ in range(4) for w in cols],
        in_specs=[any_, vm] + [any_] * 6,
        out_specs=[vm] + [any_] * 12,
        scratch_shapes=[
            pltpu.VMEM((tokens, d), BF16),
            *[pltpu.VMEM((3, tokens, w), BF16) for w in cols],
            *[pltpu.VMEM((3, tokens, w), BF16) for w in cols],
            pltpu.VMEM((3, 3, *meta.shape), F32),
            pltpu.VMEM((N, N, N, SUB, d), BF16),
            pltpu.VMEM((d, ff), BF16),
            pltpu.VMEM((d, ff), BF16),
            pltpu.VMEM((chunks, N, N, N, SUB, d), BF16),
            pltpu.VMEM((chunks, N, N, N, SUB, d), BF16),
            pltpu.VMEM((rows, ff), BF16),
            pltpu.VMEM((tokens, d), F32),
            pltpu.VMEM((2, d, u_tile), BF16),
            pltpu.VMEM((2, d, u_tile), BF16),
            pltpu.VMEM((2, u_tile, d), BF16),
            dma(()), dma((3,)), dma((2, 3)), dma((3,)),
            dma((3, 3)), dma((3, 3)), dma((3, 3)), dma((3, 3)),
            *phase, dma((3,)),
            *phase, dma((3, chunks)),
            *phase, dma((3, chunks)),
            *phase, dma((3, chunks, 4)),
            dma((3, 3)), dma((3, 3)),
        ],
        compiler_params=pltpu.CompilerParams(collective_id=0, has_side_effects=True, vmem_limit_bytes=cfg["vmem"]),
        name="moe_layer",
    )(x, meta, w_gate, w_up, w_down.reshape(chunks, N, N, N, SUB, d), s_gate, s_up, s_down)
    return outs[0]


def configure(x, expert, w_gate, s_gate):
    tokens, d = x.shape[-2:]
    top, ff, width, experts = expert.shape[-1], w_gate.shape[-1], s_gate.shape[-1], N * N * N
    slots = 5 * tokens * top // (4 * experts)
    lanes = d // 128
    cols = tuple(128 * ((lanes + 2 - r) // 3) for r in range(3))
    return dict(tokens=tokens, top=top, slots=slots, chunks=slots // SUB, cols=cols, ff=ff, f_tile=512, d_tile=256,
                units=width // 512, u_tile=512, plan=(6, 3, 8), vmem=67043328)


def solution(mesh):
    def step(x, expert, slot, gate, w_gate, w_up, w_down, s_gate, s_up, s_down):
        cfg = configure(x, expert, w_gate, s_gate)
        kept = slot[0, 0] < cfg["slots"]
        code = jnp.where(kept, expert[0, 0] * cfg["slots"] + slot[0, 0], -1).astype(F32)
        weight = gate[0, 0].astype(BF16).astype(F32)
        meta = jnp.concatenate([code.T, weight.T])
        y = layer(x[0, 0], meta, w_gate[0], w_up[0], w_down[0], s_gate, s_up, s_down, cfg)
        return y[None, None]

    tok, own, whole = P("dp", "ep", None, None), P("ep", None, None), P(None, None)
    return jax.shard_map(step, mesh=mesh, in_specs=(tok,) * 4 + (own,) * 3 + (whole,) * 3, out_specs=tok, check_vma=False)
```

time: 431 us -> 246 us (0.57)
  the two profiles are of different devices: /device:TPU:39 before, /device:TPU:1 now
where the time goes in v1:
time: 246 us; the launch traced here: 245 us
  Pallas kernels  241 us (98%)
    pallas_call x1, Pallas kernels, layer(): pl.pallas_call(functools.partial(kernel, cfg), out_shape=[jax.ShapeDtypeS...  241 us

profile of v1, /device:TPU:1, one launch (start us, length us, event | category | flops | bytes accessed | tf_op | source)
XLA Modules:
  0.0 245.4 jit_solution(1882231021955411245)
XLA Ops:
  0.0 0.7 convert_bitcast_fusion.1
  0.7 0.7 convert_bitcast_fusion
  1.4 0.6 pad_maximum_fusion.refs_1_
  2.0 241.2 %moe_layer.1 = (bf16[256,1792]{1,0:T(8,128)(2,1)}, bf16[5,4,4,4,8,640]{5,4,3,2,1,0:T(8,128)(2,1)}, bf16[5,4,4,4,8,640]{5,4,3,2,1,0:T(8,128)(2,1)}, bf16[5,4,4,4,...) custom-call(bf16[256,1792]{1,0:T(8,128)(2,1)} %bitcast.17, ...), custom_call_target="tpu_custom_call" | custom-call | tf_op jit(solution)/shard_map/moe_layer/pallas_call | solution.py:318
  243.3 2.2 copy.12

commit v2 on v0

v2 whole, which is shorter than its diff:
```python
import functools

import jax
import jax.numpy as jnp
from jax import lax
from jax.experimental import pallas as pl
from jax.experimental.pallas import tpu as pltpu
from jax.sharding import PartitionSpec as P

MESH = pl.DeviceIdType.MESH
N = 4
STRIDE = (16, 4, 1)
TURNS = ((0, 1, 2), (1, 2, 0), (2, 0, 1))
SUB = 8
ORDER = (2, 1, 3, 0)
HOPS = tuple((r, s) for s in (1, 3, 2) for r in range(3))
F32, BF16 = jnp.float32, jnp.bfloat16


def dot(a, b):
    return jnp.dot(a, b, preferred_element_type=F32)


def any_of(i, places):
    hit = i == places[0]
    for p in places[1:]:
        hit = hit | (i == p)
    return hit


def before(i, places):
    return sum((i > p).astype(jnp.int32) for p in places)


def kernel(cfg, *refs):
    tokens, chunks, cols, ff, f_tile, units, u_tile, top, slots, plan = (
        cfg[n] for n in ("tokens", "chunks", "cols", "ff", "f_tile", "units", "u_tile", "top", "slots", "plan"))
    it = iter(refs)
    take = lambda n: [next(it) for _ in range(n)]
    x_hbm, expert_ref, slot_ref, gate_ref, wg_hbm, wu_hbm, wd_hbm, sg_hbm, su_hbm, sd_hbm = take(10)
    sum_hbm, eal = take(2)
    made, bl, ecl, ebl = take(3), take(3), take(3), take(3)
    (xv,) = take(1)
    al = take(3)
    met, stage, wg, wu, wd, z, h, acc, sg, su, sd, act = take(12)
    (x_sem, w_sem, s_sem, st_sem, out_sem, a_send, a_recv, m_send, m_recv, b0_send, b0_recv, b_send, b_recv, b_self,
     c_send, c_recv, c_self, ec_send, ec_recv, ec_self, ecx_send, ecx_recv, ecx_self, eb_send, eb_recv,
     ebx_send, ebx_recv, ebx_self, ld_sem, ea_send, ea_recv) = take(31)

    me = lax.axis_index("ep")
    co = (me // 16, lax.rem(me // 4, 4), lax.rem(me, 4))
    starts = [sum(cols[:r]) for r in range(3)]
    span = [pl.ds(starts[r], cols[r]) for r in range(3)]
    d, last = sum(cols), chunks - 1
    a_axis, b_axis, c_axis = ([t[i] for t in TURNS] for i in range(3))

    def hop(c, s):
        return lax.rem(c + s, N)

    def peer(axis, s):
        return {"ep": me + (hop(co[axis], s) - co[axis]) * STRIDE[axis]}

    def remote(src, dst, send, recv, to):
        return pltpu.make_async_remote_copy(
            src_ref=src, dst_ref=dst, send_sem=send, recv_sem=recv, device_id=to, device_id_type=MESH)

    def ab(ref, r, k, a, b):
        return ref.at[k, b, a] if a_axis[r] > b_axis[r] else ref.at[k, a, b]

    def at_c(ref, r, k, c):
        if c_axis[r] == 0:
            return ref.at[k, c, :, :, :, span[r]]
        if c_axis[r] == 1:
            return ref.at[k, :, c, :, :, span[r]]
        return ref.at[k, :, :, c, :, span[r]]

    def at_ca(ref, r, k, c, a):
        ix = {c_axis[r]: c, a_axis[r]: a, b_axis[r]: slice(None)}
        return ref.at[k, ix[0], ix[1], ix[2], :, span[r]]

    every, others = slice(None), pl.ds(1, 3)

    def a_copy(r, s):
        return remote(x_hbm.at[:, span[r]], al[r].at[3 - s], a_send.at[r, 3 - s], a_recv.at[r, 3 - s], peer(a_axis[r], s))

    def m_copy(axis, s):
        return remote(met.at[axis, 0], met.at[axis, N - s], m_send.at[axis, 3 - s], m_recv.at[axis, 3 - s], peer(axis, s))

    def early_copies(r):
        return [pltpu.make_async_copy(stage.at[pl.ds(0, chunks), :, :, :, span[r]], made[r].at[:, 0], st_sem.at[r, 0]),
                pltpu.make_async_copy(stage.at[pl.ds(0, chunks), 0, :, :, span[r]], ab(bl[r], r, every, 0, 0), st_sem.at[r, 1])]

    def b0_copy(r, s):
        return remote(made[r].at[:, 0, s], ab(bl[r], r, every, 0, N - s), b0_send.at[r, s - 1], b0_recv.at[r, s - 1], peer(b_axis[r], s))

    def stage_copies(r, k):
        return [pltpu.make_async_copy(stage.at[others, :, :, :, span[r]], made[r].at[k, others], st_sem.at[r, 0]),
                pltpu.make_async_copy(stage.at[others, 0, :, :, span[r]], ab(bl[r], r, k, others, 0), st_sem.at[r, 1])]

    def b_copy(r, k, s):
        return remote(made[r].at[k, others, s], ab(bl[r], r, k, others, N - s), b_send.at[r, k, s - 1], b_recv.at[r, k, s - 1],
                      peer(b_axis[r], s))

    def c_own(r, k):
        return pltpu.make_async_copy(bl[r].at[k, :, :, 0], at_c(z, r, k, 0), c_self.at[r, k])

    def c_copy(r, k, s):
        return remote(bl[r].at[k, :, :, s], at_c(z, r, k, N - s), c_send.at[r, k, s - 1], c_recv.at[r, k, s - 1], peer(c_axis[r], s))

    def ec_own(r, k):
        return pltpu.make_async_copy(at_c(z, r, k, 0), ecl[r].at[k, :, :, 0], ec_self.at[r, k])

    def ec_copy(r, k, s):
        return remote(at_c(z, r, k, s), ecl[r].at[k, :, :, N - s], ec_send.at[r, k, s - 1], ec_recv.at[r, k, s - 1], peer(c_axis[r], s))

    def ecx_own(r, o):
        return pltpu.make_async_copy(at_ca(z, r, last, 0, o), ab(ecl[r], r, last, o, every).at[:, 0], ecx_self.at[r, o])

    def ecx_copy(r, o, s):
        return remote(at_ca(z, r, last, s, o), ab(ecl[r], r, last, o, every).at[:, N - s], ecx_send.at[r, o, s - 1],
                      ecx_recv.at[r, o, s - 1], peer(c_axis[r], s))

    def eb_copy(r, k, s):
        return remote(ab(ecl[r], r, k, every, s), ebl[r].at[k, :, N - s], eb_send.at[r, k, s - 1], eb_recv.at[r, k, s - 1],
                      peer(b_axis[r], s))

    def ebx_own(r, o):
        return pltpu.make_async_copy(ab(ecl[r], r, last, o, 0), stage.at[o, 0, :, :, span[r]], ebx_self.at[r, o])

    def ebx_copy(r, o, s):
        return remote(ab(ecl[r], r, last, o, s), stage.at[o, N - s, :, :, span[r]], ebx_send.at[r, o, s - 1], ebx_recv.at[r, o, s - 1],
                      peer(b_axis[r], s))

    def ea_copy(r, o):
        return remote(al[r].at[o - 1], eal.at[3 - o, :, span[r]], ea_send.at[r, 3 - o], ea_recv.at[r, 3 - o], peer(a_axis[r], o))

    def load(r, k, b):
        src = ab(ecl[r], r, k, every, 0) if b == 0 else ebl[r].at[k, :, b]
        return pltpu.make_async_copy(src, wd.at[k, :, b, :, :, span[r]], ld_sem.at[r, k, b])

    def up_copies(u):
        i, w = lax.rem(u, 2), pl.ds(pl.multiple_of(u * u_tile, u_tile), u_tile)
        return [pltpu.make_async_copy(sg_hbm.at[:, w], sg.at[i], s_sem.at[i, 0]),
                pltpu.make_async_copy(su_hbm.at[:, w], su.at[i], s_sem.at[i, 1])]

    def down_copy(u):
        i, w = lax.rem(u, 2), pl.ds(pl.multiple_of(u * u_tile, u_tile), u_tile)
        return pltpu.make_async_copy(sd_hbm.at[w, :], sd.at[i], s_sem.at[i, 2])

    def shared(u):
        @pl.when(u + 1 < units)
        def _():
            for c in up_copies(u + 1):
                c.start()
        down_copy(u).start()
        for c in up_copies(u):
            c.wait()
        @pl.when(u > 0)
        def _():
            down_copy(u - 1).wait()
        i, j = lax.rem(u, 2), lax.rem(u + 1, 2)
        g = dot(xv[...], sg[i])
        up = dot(xv[...], su[i])
        acc[...] += dot(act[j], sd[j])
        act[i] = (jax.nn.silu(g) * up).astype(BF16)

    def matches(r, o, first, count, weight):
        wide = min(tokens, 128)
        i = lax.broadcasted_iota(jnp.int32, (128, wide), 0)
        b, c = (co[b_axis[r]] + (i >> 5)) & 3, (co[c_axis[r]] + (i >> 3)) & 3
        expert = co[a_axis[r]] * STRIDE[a_axis[r]] + b * STRIDE[b_axis[r]] + c * STRIDE[c_axis[r]]
        base = (expert * slots + first * SUB + (i & 7)).astype(F32)
        m = met.at[a_axis[r], o]
        out = []
        for k in range(count):
            code, line = base + float(k * SUB), []
            for t in range(0, tokens, wide):
                hit = jnp.zeros((128, wide), F32)
                for j in range(top):
                    new = m[top + j : top + j + 1, t : t + wide] if weight else 1.0
                    hit = jnp.where(m[j : j + 1, t : t + wide] == code, new, hit)
                line.append(hit.astype(BF16))
            out.append(jnp.concatenate(line, axis=1))
        return jnp.concatenate(out)

    def dispatch(k):
        for r in range(3):
            for o in (1, 3, 2):
                rows = dot(matches(r, o, k, 1, False), al[r][o - 1]).astype(BF16)
                stage[o, :, :, :, span[r]] = rows.reshape(N, N, SUB, cols[r])
        for r in range(3):
            for c in stage_copies(r, k):
                c.start()
        for r in range(3):
            for c in stage_copies(r, k):
                c.wait()
        for r, s in HOPS:
            b_copy(r, k, s).start()

    def forward_c(k):
        for r in range(3):
            for s in (1, 2, 3):
                b_copy(r, k, s).wait_recv()
        for r, s in HOPS:
            c_copy(r, k, s).start()
        for r in range(3):
            c_own(r, k).start()

    def forward_eb(k):
        for r in range(3):
            for s in (1, 2, 3):
                ec_copy(r, k, s).wait_recv()
            ec_own(r, k).wait()
        for r, s in HOPS:
            eb_copy(r, k, s).start()

    def forward_ebx(o):
        for r in range(3):
            for s in (1, 2, 3):
                ecx_copy(r, o, s).wait_recv()
            ecx_own(r, o).wait()
        for r, s in HOPS:
            ebx_copy(r, o, s).start()
        for r in range(3):
            ebx_own(r, o).start()

    rows = N * N * N * SUB

    def expert(k):
        for r in range(3):
            for s in (1, 2, 3):
                c_copy(r, k, s).wait_recv()
            c_own(r, k).wait()

        def up(f, _):
            for (ek, ef), event, arg in plan["main"]:
                pl.when((k == ek) & (f == ef))(functools.partial({"C": forward_c, "F": forward_eb}[event], arg))
            w = pl.ds(pl.multiple_of(f * f_tile, f_tile), f_tile)
            zk = z[k].reshape(rows, d)
            h[:, w] = (jax.nn.silu(dot(zk, wg[:, w])) * dot(zk, wu[:, w])).astype(BF16)
            return 0
        lax.fori_loop(0, ff // f_tile, up, 0)

        at = 0
        for r in range(3):
            w = pl.ds(at, cfg["down"][r])
            at += cfg["down"][r]
            out = dot(h[...], wd[:, :, :, :, :, w].reshape(ff, cfg["down"][r]))
            z[k, :, :, :, :, w] = out.astype(BF16).reshape(N, N, N, SUB, cfg["down"][r])

            @pl.when(k < last)
            def _():
                for s in (1, 3, 2):
                    ec_copy(r, k, s).start()
                ec_own(r, k).start()

            @pl.when(k == last)
            def _():
                for o in ORDER:
                    for s in (1, 3, 2):
                        ecx_copy(r, o, s).start()
                    ecx_own(r, o).start()

    def held(r, o):
        return (pl.ds(pl.multiple_of(lax.rem(o, 2) * (128 * chunks), 128), 128 * chunks),
                pl.ds(pl.multiple_of((2 * r + o // 2) * tokens, 128 if tokens % 128 == 0 else tokens), tokens))

    def weigh(i):
        o = ordered(i)
        for r in range(3):
            wg[held(r, o)] = matches(r, o, 0, chunks, True)

    def ordered(i):
        return jnp.where(i == 0, ORDER[0], jnp.where(i == 1, ORDER[1], jnp.where(i == 2, ORDER[2], ORDER[3])))

    def combine(i, _):
        o = ordered(i)
        for r in range(3):
            for s in (1, 2, 3):
                ebx_copy(r, o, s).wait_recv()
            ebx_own(r, o).wait()
        for r in range(3):
            weight = wg[held(r, o)]
            early = wd[0:last, pl.ds(o, 1), :, :, :, span[r]].reshape(128 * last, cols[r])
            late = stage[pl.ds(o, 1), :, :, :, span[r]].reshape(128, cols[r])
            across = (((0,), (0,)), ((), ()))
            part = lax.dot_general(weight[: 128 * last], early, across, preferred_element_type=F32)
            part += lax.dot_general(weight[128 * last :], late, across, preferred_element_type=F32)

            @pl.when(o == 0)
            def _():
                acc[:, span[r]] += part

            @pl.when(o > 0)
            def _():
                al[r][pl.ds(o - 1, 1)] = part.astype(BF16)[None]
                ea_copy(r, o).start()
        return 0

    x_in = pltpu.make_async_copy(x_hbm, xv, x_sem)
    x_in.start()
    for c in up_copies(0):
        c.start()
    code = jnp.where(slot_ref[...] < slots, expert_ref[...] * slots + slot_ref[...], -1).astype(F32)
    for axis in range(3):
        met[axis, 0, :top] = code
        met[axis, 0, top:] = gate_ref[...]
    barrier = pltpu.get_barrier_semaphore()
    for axis in range(3):
        for s in (1, 2, 3):
            pl.semaphore_signal(barrier, inc=1, device_id=peer(axis, s), device_id_type=MESH)
    acc[...] = jnp.zeros_like(acc)
    act[...] = jnp.zeros_like(act)
    sd[1] = jnp.zeros_like(sd[1])
    pl.semaphore_wait(barrier, 9)
    for s in (1, 3, 2):
        for axis in range(3):
            m_copy(axis, s).start()
        for r in range(3):
            a_copy(r, s).start()
    x_in.wait()
    for r in range(3):
        mine = dot(matches(r, 0, 0, chunks, False), xv[:, span[r]]).astype(BF16)
        stage[0:chunks, :, :, :, span[r]] = mine.reshape(chunks, N, N, SUB, cols[r])
    for r in range(3):
        for c in early_copies(r):
            c.start()
    for r in range(3):
        for c in early_copies(r):
            c.wait()
    for r, s in HOPS:
        b0_copy(r, s).start()

    def weight_copy(which, k):
        if which == 2:
            return pltpu.make_async_copy(wd_hbm.at[k], wd.at[k], w_sem.at[2, k])
        w = pl.ds(pl.multiple_of(k * (d // 4), d // 4), d // 4)
        return pltpu.make_async_copy((wg_hbm, wu_hbm)[which].at[w], (wg, wu)[which].at[w], w_sem.at[which, k])

    pieces = (4, 4, chunks)
    if plan["weights"] < 0:
        for which in range(3):
            for k in range(pieces[which]):
                weight_copy(which, k).start()

    def pre(i, _):
        first, gathers, forwards = plan["weights"], plan["gather"], plan["forward"]
        if first >= 0:
            for which in range(3):
                at = first + sum(pieces[:which])

                @pl.when((i >= at) & (i < at + pieces[which]))
                def _():
                    weight_copy(which, i - at).start()

        @pl.when(i == gathers[0])
        def _():
            for axis in range(3):
                for s in (1, 2, 3):
                    m_copy(axis, s).wait_recv()
            for r, s in HOPS:
                a_copy(r, s).wait_recv()

        @pl.when(i == forwards[0])
        def _():
            for r, s in HOPS:
                b0_copy(r, s).wait_recv()

        @pl.when(any_of(i, forwards))
        def _():
            forward_c(before(i, forwards))

        @pl.when(any_of(i, gathers))
        def _():
            dispatch(before(i, gathers))

        shared(i)
        return 0
    lax.fori_loop(0, plan["pre"], pre, 0)
    for which in range(3):
        for k in range(pieces[which]):
            weight_copy(which, k).wait()
    lax.fori_loop(0, chunks, lambda k, _: (expert(k), 0)[1], 0)

    def fetch(ks):
        for k in ks:
            for r in range(3):
                for s in (1, 2, 3):
                    eb_copy(r, k, s).wait_recv()
                for b in range(4):
                    load(r, k, b).start()

    def tail(i, _):
        @pl.when(i < 4)
        def _():
            weigh(i)

        @pl.when(i == plan["eb"])
        def _():
            forward_eb(last - 1)

        @pl.when(i == plan["fetch"])
        def _():
            fetch(range(last - 1))

        for p, o in zip(plan["ebx"], ORDER, strict=True):
            pl.when(i == p)(functools.partial(forward_ebx, o))

        @pl.when(i == plan["sums"])
        def _():
            fetch([last - 1])
            for k in range(last):
                for r in range(3):
                    for b in range(4):
                        load(r, k, b).wait()
            lax.fori_loop(0, 4, combine, 0)

        shared(i + plan["pre"])
        return 0
    lax.fori_loop(0, units - plan["pre"], tail, 0)
    down_copy(units - 1).wait()
    acc[...] += dot(act[(units - 1) % 2], sd[(units - 1) % 2])
    out = pltpu.make_async_copy(acc, sum_hbm, out_sem)
    out.start()
    for r, s in HOPS:
        ea_copy(r, s).wait_recv()

    for axis in range(3):
        for s in (1, 2, 3):
            m_copy(axis, s).wait_send()
    for r, s in HOPS:
        a_copy(r, s).wait_send()
        b0_copy(r, s).wait_send()
        ea_copy(r, s).wait_send()
        for o in range(4):
            ecx_copy(r, o, s).wait_send()
            ebx_copy(r, o, s).wait_send()

    def drain(k, _):
        for r, s in HOPS:
            b_copy(r, k, s).wait_send()
            c_copy(r, k, s).wait_send()
            @pl.when(k < last)
            def _():
                ec_copy(r, k, s).wait_send()
                eb_copy(r, k, s).wait_send()
        return 0
    lax.fori_loop(0, chunks, drain, 0)
    out.wait()


def layer(x, expert, slot, gate, w_gate, w_up, w_down, s_gate, s_up, s_down, cfg):
    tokens, chunks, cols, ff, u_tile, top = (cfg[n] for n in ("tokens", "chunks", "cols", "ff", "u_tile", "top"))
    d, rows = sum(cols), N * N * N * SUB
    hbm, vm = pl.BlockSpec(memory_space=pl.ANY), pl.BlockSpec(memory_space=pltpu.VMEM)
    block = lambda w: jax.ShapeDtypeStruct((chunks, N, N, N, SUB, w), BF16)
    dma = pltpu.SemaphoreType.DMA
    phase, single, quarter = [dma((3, chunks, 3))] * 2, [dma((3, 3))] * 2, [dma((3, 4, 3))] * 2
    outs = pl.pallas_call(
        functools.partial(kernel, cfg),
        out_shape=[jax.ShapeDtypeStruct((tokens, d), F32), jax.ShapeDtypeStruct((3, tokens, d), BF16)]
        + [block(w) for _ in range(4) for w in cols],
        in_specs=[hbm] + [vm] * 3 + [hbm] * 6,
        out_specs=[hbm] * 14,
        scratch_shapes=[
            pltpu.VMEM((tokens, d), BF16),
            *[pltpu.VMEM((3, tokens, w), BF16) for w in cols],
            pltpu.VMEM((3, 4, 2 * top, tokens), F32),
            pltpu.VMEM((max(chunks, 4), N, N, SUB, d), BF16),
            pltpu.VMEM((d, ff), BF16),
            pltpu.VMEM((d, ff), BF16),
            pltpu.VMEM((chunks, N, N, N, SUB, d), BF16),
            pltpu.VMEM((chunks, N, N, N, SUB, d), BF16),
            pltpu.VMEM((rows, ff), BF16),
            pltpu.VMEM((tokens, d), F32),
            pltpu.VMEM((2, d, u_tile), BF16),
            pltpu.VMEM((2, d, u_tile), BF16),
            pltpu.VMEM((2, u_tile, d), BF16),
            pltpu.VMEM((2, tokens, u_tile), BF16),
            dma(()), dma((3, max(chunks, 4))), dma((2, 3)), dma((3, 2)), dma(()),
            *single, *single, *single,
            *phase, dma((3, chunks)),
            *phase, dma((3, chunks)),
            *phase, dma((3, chunks)),
            *quarter, dma((3, 4)),
            *phase,
            *quarter, dma((3, 4)),
            dma((3, chunks, 4)), *single,
        ],
        compiler_params=pltpu.CompilerParams(collective_id=0, has_side_effects=True, vmem_limit_bytes=cfg["vmem"]),
        name="moe_layer",
    )(x, expert, slot, gate, w_gate, w_up, w_down.reshape(chunks, N, N, N, SUB, d), s_gate, s_up, s_down)
    total, sums = outs[:2]
    for o in range(3):
        total += sums[o].astype(F32)
    return total.astype(BF16)


PLAN = {
    "pre": 18, "weights": 1, "gather": (8, 9, 10, 13, 15), "forward": (13, 15, 16),
    "main": (((0, 3), "C", 3), ((1, 1), "C", 4), ((2, 3), "F", 0), ((3, 3), "F", 1), ((4, 2), "F", 2)),
    "fetch": 1, "eb": 2, "ebx": (7, 8, 9, 10), "sums": 14,
}


def configure(x, expert, w_gate, s_gate):
    tokens, d = x.shape[-2:]
    top, ff, width, experts = expert.shape[-1], w_gate.shape[-1], s_gate.shape[-1], N * N * N
    slots = 5 * tokens * top // (4 * experts)
    lanes = d // 128
    cols = tuple(128 * ((lanes + 2 - r) // 3) for r in range(3))
    return dict(tokens=tokens, top=top, slots=slots, chunks=slots // SUB, cols=cols, ff=ff, f_tile=512, down=(768, 512, 512),
                units=width // 512, u_tile=512, plan=PLAN, vmem=67043328)


TEST = dict(
    cols=(256, 256, 128), down=(256, 256, 128),
    plan={"pre": 2, "weights": -9, "gather": (0, 1), "forward": (1,), "main": (((0, 1), "C", 1),),
          "fetch": 0, "eb": 0, "ebx": (1, 2, 3, 3), "sums": 4})


def solution(mesh):
    def step(x, expert, slot, gate, w_gate, w_up, w_down, s_gate, s_up, s_down):
        cfg = configure(x, expert, w_gate, s_gate)
        y = layer(x[0, 0], expert[0, 0].T, slot[0, 0].T, gate[0, 0].T, w_gate[0], w_up[0], w_down[0], s_gate, s_up, s_down, cfg)
        return y[None, None]

    tok, own, whole = P("dp", "ep", None, None), P("ep", None, None), P(None, None)
    return jax.shard_map(step, mesh=mesh, in_specs=(tok,) * 4 + (own,) * 3 + (whole,) * 3, out_specs=tok, check_vma=False)
```

time: 431 us -> 213 us (0.49)
  the two profiles are of different devices: /device:TPU:39 before, /device:TPU:1 now
where the time goes in v2:
time: 213 us
  Pallas kernels  210 us (99%)
  other arithmetic  3.6 us (2%)
    pallas_call x1, Pallas kernels, layer(): pl.pallas_call(functools.partial(kernel, cfg), out_shape=[jax.ShapeDtypeS...  210 us

profile of v2, /device:TPU:1, one launch (start us, length us, event | category | flops | bytes accessed | tf_op | source)
XLA Modules:
  0.0 213.3 jit_solution(18214459118715918054)
XLA Ops:
  0.0 209.7 %moe_layer.1 = (f32[256,1792]{1,0:T(8,128)}, bf16[3,256,1792]{2,1,0:T(8,128)(2,1)}, bf16[5,4,4,4,8,640]{5,4,3,2,1,0:T(8,128)(2,1)}, bf16[5,4,4,4,8,640]{5,4,3,2,...) custom-call(bf16[256,1792]{1,0:T(8,128)(2,1)} %bitcast.27, ...), custom_call_target="tpu_custom_call" | custom-call | tf_op jit(solution)/shard_map/moe_layer/pallas_call | solution.py:459
  209.7 3.6 %fusion.1 = bf16[1,1,256,1792]{3,2,1,0:T(8,128)(2,1)} fusion(f32[256,1792]{1,0:T(8,128)} %get-tuple-element.7, bf16[3,256,1792]{2,1,0:T(8,128)(2,1)} %get-tuple-element.8), kind=kLoop, calls=%fused_computation.4 | loop fusion | flops 3211264 | bytes 5505024 | tf_op jit(solution)/shard_map/broadcast_in_dim | solution.py:526

commit v3 on v2

--- a/solution.py
+++ b/solution.py
@@ -139,7 +139,7 @@
         return pltpu.make_async_copy(src, wd.at[k, :, b, :, :, span[r]], ld_sem.at[r, k, b])
 
     def up_copies(u):
-        i, w = lax.rem(u, 2), pl.ds(pl.multiple_of(u * u_tile, u_tile), u_tile)
+        i, w = lax.rem(u, 3), pl.ds(pl.multiple_of(u * u_tile, u_tile), u_tile)
         return [pltpu.make_async_copy(sg_hbm.at[:, w], sg.at[i], s_sem.at[i, 0]),
                 pltpu.make_async_copy(su_hbm.at[:, w], su.at[i], s_sem.at[i, 1])]
 
@@ -148,21 +148,21 @@
         return pltpu.make_async_copy(sd_hbm.at[w, :], sd.at[i], s_sem.at[i, 2])
 
     def shared(u):
-        @pl.when(u + 1 < units)
-        def _():
-            for c in up_copies(u + 1):
+        down_copy(u).start()
+        @pl.when(u + 2 < units)
+        def _():
+            for c in up_copies(u + 2):
                 c.start()
-        down_copy(u).start()
         for c in up_copies(u):
             c.wait()
         @pl.when(u > 0)
         def _():
             down_copy(u - 1).wait()
-        i, j = lax.rem(u, 2), lax.rem(u + 1, 2)
+        i, old = lax.rem(u, 3), lax.rem(u + 1, 2)
         g = dot(xv[...], sg[i])
         up = dot(xv[...], su[i])
-        acc[...] += dot(act[j], sd[j])
-        act[i] = (jax.nn.silu(g) * up).astype(BF16)
+        acc[...] += dot(act[...], sd[old])
+        act[...] = (jax.nn.silu(g) * up).astype(BF16)
 
     def matches(r, o, first, count, weight):
         wide = min(tokens, 128)
@@ -299,8 +299,9 @@
 
     x_in = pltpu.make_async_copy(x_hbm, xv, x_sem)
     x_in.start()
-    for c in up_copies(0):
-        c.start()
+    for u in range(2):
+        for c in up_copies(u):
+            c.start()
     code = jnp.where(slot_ref[...] < slots, expert_ref[...] * slots + slot_ref[...], -1).astype(F32)
     for axis in range(3):
         met[axis, 0, :top] = code
@@ -419,7 +420,7 @@
         return 0
     lax.fori_loop(0, units - plan["pre"], tail, 0)
     down_copy(units - 1).wait()
-    acc[...] += dot(act[(units - 1) % 2], sd[(units - 1) % 2])
+    acc[...] += dot(act[...], sd[(units - 1) % 2])
     out = pltpu.make_async_copy(acc, sum_hbm, out_sem)
     out.start()
     for r, s in HOPS:
@@ -473,11 +474,11 @@
             pltpu.VMEM((chunks, N, N, N, SUB, d), BF16),
             pltpu.VMEM((rows, ff), BF16),
             pltpu.VMEM((tokens, d), F32),
-            pltpu.VMEM((2, d, u_tile), BF16),
-            pltpu.VMEM((2, d, u_tile), BF16),
+            pltpu.VMEM((3, d, u_tile), BF16),
+            pltpu.VMEM((3, d, u_tile), BF16),
             pltpu.VMEM((2, u_tile, d), BF16),
-            pltpu.VMEM((2, tokens, u_tile), BF16),
-            dma(()), dma((3, max(chunks, 4))), dma((2, 3)), dma((3, 2)), dma(()),
+            pltpu.VMEM((tokens, u_tile), BF16),
+            dma(()), dma((3, max(chunks, 4))), dma((3, 3)), dma((3, 2)), dma(()),
             *single, *single, *single,
             *phase, dma((3, chunks)),
             *phase, dma((3, chunks)),

time: 213 us -> 201 us (0.944)
  Pallas kernels: 210 us -> 197 us
    pallas_call x1, Pallas kernels: 210 us -> 197 us  [layer(): pl.pallas_call(functools.partial(kernel, cfg), out_shape=[jax.ShapeDtypeS...]
where the time goes in v3:
time: 201 us; the launch traced here: 200 us
  Pallas kernels  197 us (98%)
  other arithmetic  3.6 us (2%)
    pallas_call x1, Pallas kernels, layer(): pl.pallas_call(functools.partial(kernel, cfg), out_shape=[jax.ShapeDtypeS...  197 us

profile of v3, /device:TPU:1, one launch (start us, length us, event | category | flops | bytes accessed | tf_op | source)
XLA Modules:
  0.0 200.5 jit_solution(8200525024250368110)
XLA Ops:
  0.0 196.9 %moe_layer.1 = (f32[256,1792]{1,0:T(8,128)}, bf16[3,256,1792]{2,1,0:T(8,128)(2,1)}, bf16[5,4,4,4,8,640]{5,4,3,2,1,0:T(8,128)(2,1)}, bf16[5,4,4,4,8,640]{5,4,3,2,...) custom-call(bf16[256,1792]{1,0:T(8,128)(2,1)} %bitcast.27, ...), custom_call_target="tpu_custom_call" | custom-call | tf_op jit(solution)/shard_map/moe_layer/pallas_call | solution.py:460
  196.9 3.6 %fusion.1 = bf16[1,1,256,1792]{3,2,1,0:T(8,128)(2,1)} fusion(f32[256,1792]{1,0:T(8,128)} %get-tuple-element.7, bf16[3,256,1792]{2,1,0:T(8,128)(2,1)} %get-tuple-element.8), kind=kLoop, calls=%fused_computation.4 | loop fusion | flops 3211264 | bytes 5505024 | tf_op jit(solution)/shard_map/broadcast_in_dim | solution.py:527

commit v4 on v3

--- a/solution.py
+++ b/solution.py
@@ -87,8 +87,8 @@
         return remote(met.at[axis, 0], met.at[axis, N - s], m_send.at[axis, 3 - s], m_recv.at[axis, 3 - s], peer(axis, s))
 
     def early_copies(r):
-        return [pltpu.make_async_copy(stage.at[pl.ds(0, chunks), :, :, :, span[r]], made[r].at[:, 0], st_sem.at[r, 0]),
-                pltpu.make_async_copy(stage.at[pl.ds(0, chunks), 0, :, :, span[r]], ab(bl[r], r, every, 0, 0), st_sem.at[r, 1])]
+        return [pltpu.make_async_copy(wd.at[:, 0, :, :, :, span[r]], made[r].at[:, 0], st_sem.at[r, 0]),
+                pltpu.make_async_copy(wd.at[:, 0, 0, :, :, span[r]], ab(bl[r], r, every, 0, 0), st_sem.at[r, 1])]
 
     def b0_copy(r, s):
         return remote(made[r].at[:, 0, s], ab(bl[r], r, every, 0, N - s), b0_send.at[r, s - 1], b0_recv.at[r, s - 1], peer(b_axis[r], s))
@@ -147,7 +147,7 @@
         i, w = lax.rem(u, 2), pl.ds(pl.multiple_of(u * u_tile, u_tile), u_tile)
         return pltpu.make_async_copy(sd_hbm.at[w, :], sd.at[i], s_sem.at[i, 2])
 
-    def shared(u):
+    def shared(u, beside=None):
         down_copy(u).start()
         @pl.when(u + 2 < units)
         def _():
@@ -159,38 +159,46 @@
         def _():
             down_copy(u - 1).wait()
         i, old = lax.rem(u, 3), lax.rem(u + 1, 2)
+        beside = beside or (lambda r: None)
         g = dot(xv[...], sg[i])
+        beside(0)
         up = dot(xv[...], su[i])
+        beside(1)
         acc[...] += dot(act[...], sd[old])
         act[...] = (jax.nn.silu(g) * up).astype(BF16)
+        beside(2)
 
     def matches(r, o, first, count, weight):
-        wide = min(tokens, 128)
-        i = lax.broadcasted_iota(jnp.int32, (128, wide), 0)
-        b, c = (co[b_axis[r]] + (i >> 5)) & 3, (co[c_axis[r]] + (i >> 3)) & 3
-        expert = co[a_axis[r]] * STRIDE[a_axis[r]] + b * STRIDE[b_axis[r]] + c * STRIDE[c_axis[r]]
-        base = (expert * slots + first * SUB + (i & 7)).astype(F32)
         m = met.at[a_axis[r], o]
+        code = m[:top].astype(jnp.int32)
+        at = [(code >> (10 - 2 * axis)) & 3 for axis in range(3)]
+        here = (code >= 0) & (at[a_axis[r]] == co[a_axis[r]])
+        place = ((at[b_axis[r]] - co[b_axis[r]]) & 3) * 32 + ((at[c_axis[r]] - co[c_axis[r]]) & 3) * 8 + (code & 7)
+        chunk = jnp.where(here, (code & 63) >> 3, -1)
+        spread = lambda v, j: jnp.broadcast_to(v[j : j + 1], (16, tokens)).astype(BF16)[None]
+        given = [spread(m[top:], j) for j in range(top)] if weight else [jnp.ones((1, 16, tokens), BF16)] * top
+        row = (lax.broadcasted_iota(jnp.int32, (8, 16, tokens), 0) * 16 + lax.broadcasted_iota(jnp.int32, (8, 16, tokens), 1))
+        row = row.astype(F32).astype(BF16)
         out = []
         for k in range(count):
-            code, line = base + float(k * SUB), []
-            for t in range(0, tokens, wide):
-                hit = jnp.zeros((128, wide), F32)
-                for j in range(top):
-                    new = m[top + j : top + j + 1, t : t + wide] if weight else 1.0
-                    hit = jnp.where(m[j : j + 1, t : t + wide] == code, new, hit)
-                line.append(hit.astype(BF16))
-            out.append(jnp.concatenate(line, axis=1))
-        return jnp.concatenate(out)
-
-    def dispatch(k):
-        for r in range(3):
-            for o in (1, 3, 2):
-                rows = dot(matches(r, o, k, 1, False), al[r][o - 1]).astype(BF16)
-                stage[o, :, :, :, span[r]] = rows.reshape(N, N, SUB, cols[r])
+            mine = jnp.where(chunk == first + k, place, -1).astype(F32)
+            hit = jnp.zeros((8, 16, tokens), BF16)
+            for j in range(top):
+                hit = jnp.where(spread(mine, j) == row, given[j], hit)
+            out.append(hit.reshape(128, tokens))
+        return jnp.concatenate(out) if count > 1 else out[0]
+
+    def gather(k, r):
+        for o in (1, 3, 2):
+            rows = dot(matches(r, o, k, 1, False), al[r][o - 1]).astype(BF16)
+            stage[o, :, :, :, span[r]] = rows.reshape(N, N, SUB, cols[r])
+
+    def keep(k):
         for r in range(3):
             for c in stage_copies(r, k):
                 c.start()
+
+    def dispatch(k):
         for r in range(3):
             for c in stage_copies(r, k):
                 c.wait()
@@ -262,13 +270,12 @@
                     ecx_own(r, o).start()
 
     def held(r, o):
-        return (pl.ds(pl.multiple_of(lax.rem(o, 2) * (128 * chunks), 128), 128 * chunks),
-                pl.ds(pl.multiple_of((2 * r + o // 2) * tokens, 128 if tokens % 128 == 0 else tokens), tokens))
-
-    def weigh(i):
+        wide = 128 * chunks
+        return pl.ds(r * tokens, tokens), pl.ds(pl.multiple_of(o * wide, wide), wide)
+
+    def weigh(i, r):
         o = ordered(i)
-        for r in range(3):
-            wg[held(r, o)] = matches(r, o, 0, chunks, True)
+        wg[held(r, o)] = matches(r, o, 0, chunks, True).T
 
     def ordered(i):
         return jnp.where(i == 0, ORDER[0], jnp.where(i == 1, ORDER[1], jnp.where(i == 2, ORDER[2], ORDER[3])))
@@ -283,9 +290,7 @@
             weight = wg[held(r, o)]
             early = wd[0:last, pl.ds(o, 1), :, :, :, span[r]].reshape(128 * last, cols[r])
             late = stage[pl.ds(o, 1), :, :, :, span[r]].reshape(128, cols[r])
-            across = (((0,), (0,)), ((), ()))
-            part = lax.dot_general(weight[: 128 * last], early, across, preferred_element_type=F32)
-            part += lax.dot_general(weight[128 * last :], late, across, preferred_element_type=F32)
+            part = dot(weight[:, : 128 * last], early) + dot(weight[:, 128 * last :], late)
 
             @pl.when(o == 0)
             def _():
@@ -302,7 +307,7 @@
     for u in range(2):
         for c in up_copies(u):
             c.start()
-    code = jnp.where(slot_ref[...] < slots, expert_ref[...] * slots + slot_ref[...], -1).astype(F32)
+    code = jnp.where(slot_ref[...] < slots, expert_ref[...] * 64 + slot_ref[...], -1).astype(F32)
     for axis in range(3):
         met[axis, 0, :top] = code
         met[axis, 0, top:] = gate_ref[...]
@@ -322,7 +327,7 @@
     x_in.wait()
     for r in range(3):
         mine = dot(matches(r, 0, 0, chunks, False), xv[:, span[r]]).astype(BF16)
-        stage[0:chunks, :, :, :, span[r]] = mine.reshape(chunks, N, N, SUB, cols[r])
+        wd[:, 0, :, :, :, span[r]] = mine.reshape(chunks, N, N, SUB, cols[r])
     for r in range(3):
         for c in early_copies(r):
             c.start()
@@ -354,6 +359,10 @@
                 def _():
                     weight_copy(which, i - at).start()
 
+        @pl.when(any_of(i - 1, gathers))
+        def _():
+            dispatch(before(i - 1, gathers))
+
         @pl.when(i == gathers[0])
         def _():
             for axis in range(3):
@@ -371,11 +380,17 @@
         def _():
             forward_c(before(i, forwards))
 
-        @pl.when(any_of(i, gathers))
-        def _():
-            dispatch(before(i, gathers))
-
-        shared(i)
+        gathering = any_of(i, gathers)
+
+        @pl.when(gathering)
+        def _():
+            k = before(i, gathers)
+            shared(i, lambda r: gather(k, r))
+            keep(k)
+
+        @pl.when(jnp.logical_not(gathering))
+        def _():
+            shared(i)
         return 0
     lax.fori_loop(0, plan["pre"], pre, 0)
     for which in range(3):
@@ -391,15 +406,16 @@
                 for b in range(4):
                     load(r, k, b).start()
 
+    def masks(i, _):
+        @pl.when(i == plan["eb"])
+        def _():
+            forward_eb(last - 1)
+
+        shared(i + plan["pre"], lambda r: weigh(i, r))
+        return 0
+    lax.fori_loop(0, 4, masks, 0)
+
     def tail(i, _):
-        @pl.when(i < 4)
-        def _():
-            weigh(i)
-
-        @pl.when(i == plan["eb"])
-        def _():
-            forward_eb(last - 1)
-
         @pl.when(i == plan["fetch"])
         def _():
             fetch(range(last - 1))
@@ -418,7 +434,7 @@
 
         shared(i + plan["pre"])
         return 0
-    lax.fori_loop(0, units - plan["pre"], tail, 0)
+    lax.fori_loop(4, units - plan["pre"], tail, 0)
     down_copy(units - 1).wait()
     acc[...] += dot(act[...], sd[(units - 1) % 2])
     out = pltpu.make_async_copy(acc, sum_hbm, out_sem)
@@ -467,7 +483,7 @@
             pltpu.VMEM((tokens, d), BF16),
             *[pltpu.VMEM((3, tokens, w), BF16) for w in cols],
             pltpu.VMEM((3, 4, 2 * top, tokens), F32),
-            pltpu.VMEM((max(chunks, 4), N, N, SUB, d), BF16),
+            pltpu.VMEM((N, N, N, SUB, d), BF16),
             pltpu.VMEM((d, ff), BF16),
             pltpu.VMEM((d, ff), BF16),
             pltpu.VMEM((chunks, N, N, N, SUB, d), BF16),
@@ -498,9 +514,9 @@
 
 
 PLAN = {
-    "pre": 18, "weights": 1, "gather": (8, 9, 10, 13, 15), "forward": (13, 15, 16),
-    "main": (((0, 3), "C", 3), ((1, 1), "C", 4), ((2, 3), "F", 0), ((3, 3), "F", 1), ((4, 2), "F", 2)),
-    "fetch": 1, "eb": 2, "ebx": (7, 8, 9, 10), "sums": 14,
+    "pre": 21, "weights": 1, "gather": (7, 8, 9, 13, 16), "forward": (12, 16, 18),
+    "main": (((0, 3), "C", 3), ((1, 2), "C", 4), ((2, 3), "F", 0), ((3, 3), "F", 1), ((4, 3), "F", 2)),
+    "eb": 3, "ebx": (6, 8, 9, 9), "fetch": 12, "sums": 13,
 }
 
 
@@ -516,8 +532,8 @@
 
 TEST = dict(
     cols=(256, 256, 128), down=(256, 256, 128),
-    plan={"pre": 2, "weights": -9, "gather": (0, 1), "forward": (1,), "main": (((0, 1), "C", 1),),
-          "fetch": 0, "eb": 0, "ebx": (1, 2, 3, 3), "sums": 4})
+    plan={"pre": 3, "weights": -9, "gather": (0, 1), "forward": (2,), "main": (((0, 1), "C", 1),),
+          "eb": 0, "ebx": (4, 4, 5, 5), "fetch": 5, "sums": 6})
 
 
 def solution(mesh):

time: 201 us -> 193 us (0.960)
  Pallas kernels: 197 us -> 189 us
    pallas_call x1, Pallas kernels: 197 us -> 189 us  [layer(): pl.pallas_call(functools.partial(kernel, cfg), out_shape=[jax.ShapeDtypeS...]
where the time goes in v4:
time: 193 us
  Pallas kernels  189 us (98%)
  other arithmetic  3.6 us (2%)
    pallas_call x1, Pallas kernels, layer(): pl.pallas_call(functools.partial(kernel, cfg), out_shape=[jax.ShapeDtypeS...  189 us

profile of v4, /device:TPU:1, one launch (start us, length us, event | category | flops | bytes accessed | tf_op | source)
XLA Modules:
  0.0 192.6 jit_solution(14909626853708089320)
XLA Ops:
  0.0 189.0 %moe_layer.1 = (f32[256,1792]{1,0:T(8,128)}, bf16[3,256,1792]{2,1,0:T(8,128)(2,1)}, bf16[5,4,4,4,8,640]{5,4,3,2,1,0:T(8,128)(2,1)}, bf16[5,4,4,4,8,640]{5,4,3,2,...) custom-call(bf16[256,1792]{1,0:T(8,128)(2,1)} %bitcast.27, ...), custom_call_target="tpu_custom_call" | custom-call | tf_op jit(solution)/shard_map/moe_layer/pallas_call | solution.py:476
  189.0 3.6 %fusion.1 = bf16[1,1,256,1792]{3,2,1,0:T(8,128)(2,1)} fusion(f32[256,1792]{1,0:T(8,128)} %get-tuple-element.7, bf16[3,256,1792]{2,1,0:T(8,128)(2,1)} %get-tuple-element.8), kind=kLoop, calls=%fused_computation.4 | loop fusion | flops 3211264 | bytes 5505024 | tf_op jit(solution)/shard_map/broadcast_in_dim | solution.py:543
